TPU v7x, 128 devices: a whole 4x4x4 slice. The times are simulated.
128 devices in a mesh: grp: 4 (over z), kv: 16 (over x, y), tp: 2 (over core).
Axes of the slice: x: 4, y: 4, z: 4, core: 2. Of those that a mesh axis runs over, the one named last changes fastest.
Arguments:
- hidden_states: bfloat16 [512, 4096], P('grp', 'kv'), may hold values from -6 to 6
- attn_gain: float32 [4096], P('kv'), may hold values from 0.25 to 1.75
- mlp_gain: float32 [4096], replicated, may hold values from 0.25 to 1.75
- w_query: bfloat16 [4096, 4096], P('kv', 'tp'), may hold values from -0.09375 to 0.09375
- w_out: bfloat16 [32, 128, 4096], P('tp', 'kv'), may hold values from -1 to 1
- w_gate: bfloat16 [4096, 14336], P(None, ('kv', 'tp')), may hold values from -0.09375 to 0.09375
- w_up: bfloat16 [4096, 14336], P(None, ('kv', 'tp')), may hold values from -0.09375 to 0.09375
- w_down: bfloat16 [14336, 4096], P(('kv', 'tp')), may hold values from -0.046875 to 0.046875
- kv_pool: bfloat16 [1024, 2, 128, 1024], P(('grp', 'kv'), None, None, 'tp'), may hold values from -110 to 110
- resident_cache: bfloat16 [4, 128, 2, 128, 1024], P('grp', 'kv', None, None, 'tp'), may hold values from -110 to 110
- resident_slot: int32 [4, 128], P('grp', 'kv'), may hold values from 0 to 127
- resident_len: int32 [4, 128], P('grp', 'kv'), may hold values from 1 to 128
- new_owner: int32 [4, 256], replicated, may hold values from 0 to 63, as said below
- new_local: int32 [4, 256], replicated, may hold values from 0 to 15
- new_slot: int32 [4, 256], P('grp', 'kv'), may hold values from 0 to 127
- new_len: int32 [4, 256], P('grp', 'kv'), may hold values from 1 to 128
- token_kv: bfloat16 [512, 2, 1024], P('grp', None, 'tp'), may hold values from -6 to 6
Outputs:
- mixed: bfloat16 [512, 4096], P(('grp', 'kv', 'tp'))
- new_cache: bfloat16 [4, 256, 2, 128, 1024], P('grp', 'kv', None, None, 'tp')
Inputs may be any that keep to these rules, and one draw needn't show every extreme that they name: New page c of group g is kept by the device of kv index c // 16 of group g and comes from the device whose index along grp+kv is new_owner[g, c]; every decode device receives exactly 4 new pages from the owners of each grp index; no owner sends more than 1 pages to the devices of one kv index over all groups, so at most 1 to one device; every owner sends each of its 16 pages exactly once.
All inputs are finite; a program needn't handle non-finite values.
Results may differ from a plain program's by a relative error of at most 0.018.
Values may be sent and summed in bfloat16 or wider, within the bound.
A program may use at most 128 MiB of HBM per device.

v0:
```python
import jax
import jax.numpy as jnp
from jax import lax
from jax.sharding import Mesh
from jax.sharding import PartitionSpec as P

D = 4096
HEADS = 32
KV_HEADS = 8
HEAD_DIM = 128
NPR = 4
KV = ("kv_0", "kv_1")
KV_TP = ("kv_0", "kv_1", "tp")
GRP_KV = ("grp", "kv_0", "kv_1")
GRP_KV_TP = ("grp", "kv_0", "kv_1", "tp")
neg_fill = -1e30
norm_eps = 1e-05


def combined_by_axis(shard, axes, combine):
    for axis in axes:
        pieces = jax.tree.map(lambda part: lax.all_gather(part, axis), shard)
        shard = jax.tree.map(lambda part: part[0], pieces)
        for k in range(1, lax.axis_size(axis)):
            shard = combine(shard, jax.tree.map(lambda part: part[k], pieces))
    return shard


def split_up(shard, dim, peers):
    before, after = (shard.shape[:dim], shard.shape[dim + 1 :])
    return jnp.moveaxis(shard.reshape(*before, peers, -1, *after), dim, 0)


def summed_on_arrival(shard, axis, dim):
    tiles = split_up(shard, dim, lax.axis_size(axis))
    arrived = lax.all_to_all(tiles, axis, split_axis=0, concat_axis=0, tiled=True)
    return arrived.astype(jnp.float32).sum(axis=0)


def combine(earlier, later):
    top_a, sum_a, acc_a = earlier
    top_b, sum_b, acc_b = later
    top = jnp.maximum(top_a, top_b)
    fade_a = jnp.exp(top_a - top)
    fade_b = jnp.exp(top_b - top)
    return (
        top,
        sum_a * fade_a + sum_b * fade_b,
        acc_a * fade_a[..., None] + acc_b * fade_b[..., None],
    )


def nth_match(table, wanted, places):
    matched = (table == wanted).astype(jnp.int32)
    ranking = jnp.cumsum(matched, axis=1) - 1
    return (matched[:, None, :] == 1) & (ranking[:, None, :] == places[None, :, None])


def move_pages(kv_pool, new_owner, new_local):
    groups = lax.axis_size("grp")
    ranks = lax.axis_size(KV)
    per_dev = new_owner.shape[1] // ranks
    cap = groups * NPR // ranks
    grp_rank = lax.axis_index("grp")
    kv_rank = lax.axis_index(KV)
    owners = new_owner.reshape(groups * ranks, per_dev)
    myself = grp_rank * ranks + kv_rank
    places = jnp.arange(cap, dtype=jnp.int32)
    mine = lax.dynamic_index_in_dim(owners, myself, 0, keepdims=False)
    order = jnp.arange(per_dev, dtype=jnp.int32)
    by_col = (
        new_owner.reshape(groups, ranks, per_dev)
        .transpose(1, 0, 2)
        .reshape(ranks, groups * per_dev)
    )
    local_col = (
        new_local.reshape(groups, ranks, per_dev)
        .transpose(1, 0, 2)
        .reshape(ranks, groups * per_dev)
    )
    select = nth_match(by_col, myself, places)
    picked = jnp.sum(jnp.where(select, local_col[:, None, :], 0), axis=2)
    outgoing = jnp.take(kv_pool, picked.reshape(-1), axis=0)
    received = lax.all_to_all(outgoing, KV, split_axis=0, concat_axis=0, tiled=True)
    row_here = lax.dynamic_index_in_dim(by_col, kv_rank, 0, keepdims=False)
    sources = grp_rank * ranks + jnp.arange(ranks, dtype=jnp.int32)
    hits = nth_match(
        jnp.broadcast_to(row_here[None, :], (ranks, row_here.shape[0])), sources[:, None], places
    )
    spots = jnp.arange(row_here.shape[0], dtype=jnp.int32)
    where_f = jnp.sum(jnp.where(hits, spots[None, None, :], 0), axis=2).reshape(-1)
    dest_grp = where_f // per_dev
    dest_pos = where_f % per_dev
    same = (dest_grp[:, None] == dest_grp[None, :]) & (dest_pos[:, None] < dest_pos[None, :])
    rank_in = jnp.sum(same.astype(jnp.int32), axis=0)
    target = dest_grp * NPR + rank_in
    items = jnp.arange(target.shape[0], dtype=jnp.int32)
    inverse = jnp.sum(jnp.where(target[None, :] == items[:, None], items[None, :], 0), axis=1)
    sorted_pages = jnp.take(received, inverse, axis=0)
    arrived = lax.all_to_all(sorted_pages, "grp", split_axis=0, concat_axis=0, tiled=True)
    src_grp = mine // ranks
    earlier = (src_grp[:, None] == src_grp[None, :]) & (order[:, None] < order[None, :])
    before = jnp.sum(earlier.astype(jnp.int32), axis=0)
    return jnp.take(arrived, src_grp * NPR + before, axis=0)


def local_partials(query, resident, arrived, res_slot, res_len, arr_slot, arr_len, token_kv, first):
    pages = jnp.concatenate([resident, arrived], axis=0)
    owner_slot = jnp.concatenate([res_slot, arr_slot])
    filled = jnp.concatenate([res_len, arr_len])
    count = pages.shape[0]
    tokens = pages.shape[2]
    kv_here = pages.shape[3] // HEAD_DIM
    slots = query.shape[0]
    ratio = HEADS // KV_HEADS
    keys = pages[:, 0].astype(jnp.float32).reshape(count, tokens, kv_here, HEAD_DIM)
    values = pages[:, 1].astype(jnp.float32).reshape(count, tokens, kv_here, HEAD_DIM)
    grouped = query.reshape(slots, kv_here, ratio, HEAD_DIM)
    picked = jnp.take(grouped, owner_slot, axis=0)
    scores = jnp.einsum("ikgd,itkd->ikgt", picked, keys, precision=lax.Precision.HIGHEST)
    usable = (jnp.arange(tokens, dtype=jnp.int32)[None, :] < filled[:, None])[:, None, None, :]
    scores = jnp.where(usable, scores, neg_fill)
    page_top = jnp.max(scores, axis=3)
    member = owner_slot[None, :] == jnp.arange(slots, dtype=jnp.int32)[:, None]
    slot_top = jnp.max(jnp.where(member[:, :, None, None], page_top[None], neg_fill), axis=1)
    own_keys = token_kv[:, 0].astype(jnp.float32).reshape(slots, kv_here, HEAD_DIM)
    own_values = token_kv[:, 1].astype(jnp.float32).reshape(slots, kv_here, HEAD_DIM)
    own_score = jnp.einsum("skgd,skd->skg", grouped, own_keys, precision=lax.Precision.HIGHEST)
    own_score = jnp.where(first, own_score, neg_fill)
    slot_top = jnp.maximum(slot_top, own_score)
    reach = jnp.take(slot_top, owner_slot, axis=0)
    weights = jnp.where(usable, jnp.exp(scores - reach[..., None]), 0.0)
    page_sum = jnp.sum(weights, axis=3)
    page_acc = jnp.einsum("ikgt,itkd->ikgd", weights, values, precision=lax.Precision.HIGHEST)
    own_weight = jnp.where(first, jnp.exp(own_score - slot_top), 0.0)
    member_f = member.astype(jnp.float32)
    total = jnp.dot(member_f, page_sum.reshape(count, -1), precision=lax.Precision.HIGHEST)
    total = total + own_weight.reshape(slots, -1)
    weighted = jnp.dot(member_f, page_acc.reshape(count, -1), precision=lax.Precision.HIGHEST)
    weighted = (
        weighted.reshape(slots, kv_here, ratio, HEAD_DIM)
        + own_weight[..., None] * own_values[:, :, None, :]
    )
    return (slot_top.reshape(slots, -1), total, weighted.reshape(slots, kv_here * ratio, HEAD_DIM))


def per_device(
    hidden_states,
    attn_gain,
    mlp_gain,
    w_query,
    w_out,
    w_gate,
    w_up,
    w_down,
    kv_pool,
    resident_cache,
    resident_slot,
    resident_len,
    new_owner,
    new_local,
    new_slot,
    new_len,
    token_kv,
):
    ranks = lax.axis_size(KV)
    pairs = lax.axis_size("tp")
    kv_rank = lax.axis_index(KV)
    tp_rank = lax.axis_index("tp")
    features = hidden_states.astype(jnp.float32)
    partial_query = jnp.dot(
        (features * attn_gain).astype(jnp.bfloat16), w_query, preferred_element_type=jnp.float32
    )
    squares = jnp.sum(features * features, axis=1)
    partial_query, squares = lax.psum((partial_query, squares), KV)
    attn_scale = lax.rsqrt(squares / D + norm_eps)
    query = partial_query * attn_scale[:, None] * HEAD_DIM ** (-0.5)
    new_pages = move_pages(kv_pool, new_owner, new_local)
    top, total, weighted = local_partials(
        query,
        resident_cache[0],
        new_pages,
        resident_slot[0],
        resident_len[0],
        new_slot[0],
        new_len[0],
        token_kv,
        kv_rank == 0,
    )
    top, total, weighted = combined_by_axis((top, total, weighted), KV, combine)
    attn = (weighted / total[..., None]).astype(jnp.bfloat16)
    slots = attn.shape[0]
    heads_here = attn.shape[1]
    span = HEAD_DIM // ranks
    piece = lax.dynamic_slice_in_dim(attn, kv_rank * span, span, 2)
    branch = jnp.dot(
        piece.reshape(slots, heads_here * span),
        w_out.reshape(heads_here * span, w_out.shape[2]),
        preferred_element_type=jnp.float32,
    )
    width_here = hidden_states.shape[1]
    laid = branch.reshape(slots, ranks, width_here)
    spot = (jnp.arange(ranks, dtype=jnp.int32) == kv_rank) & (tp_rank == 0)
    laid = laid + jnp.where(spot[None, :, None], features[:, None, :], 0.0)
    resid = lax.psum(laid.reshape(slots, ranks * width_here).astype(jnp.bfloat16), KV_TP)
    resid_f = resid.astype(jnp.float32)
    mlp_scale = lax.rsqrt(jnp.sum(resid_f * resid_f, axis=1) / D + norm_eps)
    normed_mlp = (resid_f * mlp_gain).astype(jnp.bfloat16)
    gate = jnp.dot(normed_mlp, w_gate, preferred_element_type=jnp.float32) * mlp_scale[:, None]
    upward = jnp.dot(normed_mlp, w_up, preferred_element_type=jnp.float32) * mlp_scale[:, None]
    hidden_units = (jax.nn.silu(gate) * upward).astype(jnp.bfloat16)
    row_count = slots // (ranks * pairs)
    down = summed_on_arrival(
        jnp.dot(hidden_units, w_down, preferred_element_type=jnp.float32).astype(jnp.bfloat16),
        KV_TP,
        0,
    )
    row_start = (kv_rank * pairs + tp_rank) * row_count
    kept = lax.dynamic_slice_in_dim(resid_f, row_start, row_count, 0)
    mixed = (kept + down).astype(jnp.bfloat16)
    return (mixed, new_pages[None])


def solution(mesh):
    finer = Mesh(
        mesh.devices.reshape(mesh.shape["grp"], 4, 4, mesh.shape["tp"]),
        ("grp", "kv_0", "kv_1", "tp"),
    )
    return jax.shard_map(
        per_device,
        mesh=finer,
        in_specs=(
            P("grp", KV),
            P(KV),
            P(),
            P(KV, "tp"),
            P("tp", KV, None),
            P(None, KV_TP),
            P(None, KV_TP),
            P(KV_TP, None),
            P(GRP_KV, None, None, "tp"),
            P("grp", KV, None, None, "tp"),
            P("grp", KV),
            P("grp", KV),
            P(),
            P(),
            P("grp", KV),
            P("grp", KV),
            P("grp", None, "tp"),
        ),
        out_specs=(P(GRP_KV_TP, None), P("grp", KV, None, None, "tp")),
        check_vma=False,
    )
```

profile of v0, /device:TPU:1, one launch (start us, length us, event | category | flops | bytes accessed | tf_op | source)
XLA Modules:
  0.0 507.7 jit_solution(3619202428460434715)
XLA Ops:
  10.4 5.0 gather_fusion.2
  15.5 4.7 broadcast_select_fusion.2
  20.1 7.6 %all-to-all-start = ((bf16[16,2,128,512]{3,2,1,0:T(8,128)(2,1)}), bf16[16,2,128,512]{3,2,1,0:T(8,128)(2,1)}, u32[]{:S(2)}, u32[]{:S(2)}) async-start(bf16[16,2,128,512]{3,2,1,0:T(8,128)(2,1)} %broadcast_select_fusion.2), calls=%async_computation | async-start | bytes 8388608 | tf_op jit(solution)/shard_map/all_to_all | solution.py:84
  28.5 59.5 %all-to-all-done = bf16[16,2,128,512]{3,2,1,0:T(8,128)(2,1)} async-done(((bf16[16,2,128,512]{3,2,1,0:T(8,128)(2,1)}), bf16[16,2,128,512]{3,2,1,0:T(8,128)(2,1)}, u32[]{:S(2)}, u32[]{:S(2)}) %all-to-all-start) | async-done | bytes 4194336 | tf_op jit(solution)/shard_map/all_to_all | solution.py:84
  88.1 5.0 gather_fusion.3
  93.1 4.7 broadcast_select_fusion.1
  97.8 5.2 %all-to-all-start.1 = ((bf16[16,2,128,512]{3,2,1,0:T(8,128)(2,1)}), bf16[16,2,128,512]{3,2,1,0:T(8,128)(2,1)}, u32[]{:S(2)}, u32[]{:S(2)}) async-start(bf16[16,2,128,512]{3,2,1,0:T(8,128)(2,1)} %broadcast_select_fusion.1), calls=%async_computation.1 | async-start | bytes 8388608 | tf_op jit(solution)/shard_map/all_to_all | solution.py:100
  105.6 33.9 %psum.22 = f32[128]{0:T(128)S(1)} all-reduce(f32[128]{0:T(128)S(1)} %multiply_reduce_fusion.1), channel_id=1, replica_groups=mesh['grp'=4,'kv_0'=4,'kv_1'=4,'tp'=2] {'kv_0','kv_1'}, use_global_device_ids=true, to_apply=%region_2.0 | all-reduce | flops 128 | bytes 1024 | tf_op jit(solution)/shard_map/psum | solution.py:175
  139.8 61.1 %all-reduce.3.cloned.1.call-done = f32[128,2048]{1,0:T(8,128)} async-done(((f32[128,2048]{1,0:T(8,128)}), f32[128,2048]{1,0:T(8,128)}) %all-reduce.3.cloned.1.call-update) | async-done | bytes 1048592 | tf_op jit(solution)/shard_map/psum | solution.py:175
  203.7 1.8 fusion.81
  205.5 5.0 gather_fusion.4
  210.6 2.8 broadcast_select_fusion
  213.4 2.9 pad_maximum_fusion
  216.3 4.7 copy.150
  221.0 4.6 fusion.80
  227.0 4.7 copy.155
  231.7 6.9 %fusion.17 = f32[24,4,4,128]{3,2,1,0:T(4,128)S(1)} fusion(bf16[24,128,4,128]{1,3,2,0:T(8,128)(2,1)} %bitcast.217, f32[24,4,4,128]{3,2,1,0:T(4,128)S(1)} %get-tuple-element.40, f32[24,4,4]{2,1,0:T(4,128)S(1)} %broadcast_select_fusion.3, pred[24,128]{1,0:T(8,128)(4,1)S(1)} %iota_compare_fusion), kind=kOutput, calls=%fused_computation.52 | convolution fusion | flops 75595776 | bytes 3543552 | tf_op jit(solution)/shard_map/ikgt,itkd->ikgd/dot_general | solution.py:134
  241.4 9.3 %all_gather.25 = f32[4,128,16]{1,2,0:T(8,128)S(1)} all-gather(f32[1,128,16]{1,2,0:T(8,128)S(1)} %bitcast.229), channel_id=1, replica_groups=mesh['grp'=4,'kv_0'=4,'kv_1'=4,'tp'=2] {'kv_0'}, dimensions={0}, use_global_device_ids=true | all-gather | bytes 40960 | tf_op jit(solution)/shard_map/all_gather | solution.py:22
  251.3 38.9 %all-gather.4.cloned.1.call-done = f32[4,128,16,128]{3,2,1,0:T(8,128)} async-done(((f32[1,128,16,128]{3,2,1,0:T(8,128)}), f32[4,128,16,128]{3,2,1,0:T(8,128)}) %all-gather.4.cloned.1.call-update) | async-done | bytes 4194320 | tf_op jit(solution)/shard_map/all_gather | solution.py:22
  290.2 4.8 fusion.3
  297.1 9.0 %all-gather = f32[512,16]{0,1:T(8,128)S(1)} all-gather(f32[128,16]{0,1:T(8,128)S(1)} %convolution_add_fusion.1), channel_id=2, replica_groups=mesh['grp'=4,'kv_0'=4,'kv_1'=4,'tp'=2] {'kv_0'}, dimensions={0}, use_global_device_ids=true | all-gather | bytes 40960 | tf_op jit(solution)/shard_map/all_gather | solution.py:22
  306.2 10.8 %all_gather.27 = f32[4,128,16]{1,2,0:T(8,128)S(1)} all-gather(f32[1,128,16]{1,2,0:T(8,128)S(1)} %get-tuple-element.15), channel_id=1, replica_groups=mesh['grp'=4,'kv_0'=4,'kv_1'=4,'tp'=2] {'kv_1'}, dimensions={0}, use_global_device_ids=true | all-gather | bytes 40960 | tf_op jit(solution)/shard_map/all_gather | solution.py:22
  317.0 10.6 %all_gather.30 = f32[4,128,16]{1,2,0:T(8,128)S(1)} all-gather(f32[1,128,16]{1,2,0:T(8,128)S(1)} %get-tuple-element.14), channel_id=1, replica_groups=mesh['grp'=4,'kv_0'=4,'kv_1'=4,'tp'=2] {'kv_1'}, dimensions={0}, use_global_device_ids=true | all-gather | bytes 40960 | tf_op jit(solution)/shard_map/all_gather | solution.py:22
  327.6 16.7 %all-gather.6.cloned.1.call-done = f32[4,128,16,128]{3,2,1,0:T(8,128)} async-done(((f32[1,128,16,128]{3,2,1,0:T(8,128)}), f32[4,128,16,128]{3,2,1,0:T(8,128)}) %all-gather.6.cloned.1.call-update) | async-done | bytes 4194320 | tf_op jit(solution)/shard_map/all_gather | solution.py:22
  344.3 3.9 fusion.78
  350.2 2.6 copy.188
  358.2 105.7 %all-reduce.5.cloned.1.call-done = bf16[128,4096]{1,0:T(8,128)(2,1)} async-done(((bf16[128,4096]{1,0:T(8,128)(2,1)}), bf16[128,4096]{1,0:T(8,128)(2,1)}) %all-reduce.5.cloned.1.call-update) | async-done | bytes 1048592 | tf_op jit(solution)/shard_map/psum | solution.py:205
  465.5 3.5 convolution_multiply_fusion.1
  469.0 6.0 %convolution_convert_fusion = bf16[128,4096]{1,0:T(8,128)(2,1)S(1)} fusion(bf16[448,4096]{1,0:T(8,128)(2,1)} %param.26, bf16[4096,448]{0,1:T(8,128)(2,1)} %param.25, f32[4096]{0:T(1024)S(1)} %copy-done.7, bf16[128,4096]{1,0:T(8,128)(2,1)S(1)} %copy-done.2, f32[128,448]{0,1:T(8,128)S(1)} %convolution_multiply_fusion.1, f32[128]{0:T(128)S(1)} %add_rsqrt_fusion), kind=kOutput, calls=%fused_computation.7 | convolution fusion | flops 942022656 | bytes 9683456 | tf_op jit(solution)/shard_map/dot_general | solution.py:214
  476.3 6.1 %all-to-all-start.2 = ((bf16[32,4,4096]{2,1,0:T(4,128)(2,1)}), bf16[32,4,4096]{2,1,0:T(4,128)(2,1)S(1)}, u32[]{:S(2)}, u32[]{:S(2)}) async-start(bf16[32,4,4096]{2,1,0:T(4,128)(2,1)} %reshape.671), calls=%async_computation.2 | async-start | bytes 2097152 | tf_op jit(solution)/shard_map/all_to_all | solution.py:36
  482.3 4.8 fusion.92
  488.7 10.6 %all-to-all-done.2 = bf16[32,4,4096]{2,1,0:T(4,128)(2,1)S(1)} async-done(((bf16[32,4,4096]{2,1,0:T(4,128)(2,1)}), bf16[32,4,4096]{2,1,0:T(4,128)(2,1)S(1)}, u32[]{:S(2)}, u32[]{:S(2)}) %all-to-all-start.2) | async-done | bytes 1048608 | tf_op jit(solution)/shard_map/all_to_all | solution.py:36
  (121 shorter events, 30.3 us)
Async XLA Ops:
  7.2 95.8 %copy-start = (bf16[256,2048]{1,0:T(8,128)(2,1)S(1)}, bf16[256,2048]{1,0:T(8,128)(2,1)}, u32[]{:S(2)}) copy-start(bf16[256,2048]{1,0:T(8,128)(2,1)} %param.22) | copy-start | bytes 3145732
  20.1 68.0 %all-to-all-start = ((bf16[16,2,128,512]{3,2,1,0:T(8,128)(2,1)}), bf16[16,2,128,512]{3,2,1,0:T(8,128)(2,1)}, u32[]{:S(2)}, u32[]{:S(2)}) async-start(bf16[16,2,128,512]{3,2,1,0:T(8,128)(2,1)} %broadcast_select_fusion.2), calls=%async_computation | async-start | bytes 8388608 | tf_op jit(solution)/shard_map/all_to_all | solution.py:84
  97.8 5.3 %copy-start.6 = (bf16[128,256]{1,0:T(8,128)(2,1)S(1)}, bf16[128,256]{1,0:T(8,128)(2,1)}, u32[]{:S(2)}) copy-start(bf16[128,256]{1,0:T(8,128)(2,1)} %param.19) | copy-start | bytes 196612
  97.8 5.3 %copy-start.8 = (f32[256]{0:T(256)S(1)}, f32[256]{0:T(256)}, u32[]{:S(2)}) copy-start(f32[256]{0:T(256)} %param.20) | copy-start | bytes 3076
  97.8 6.7 %copy-start.9 = (s32[1,16]{1,0:T(1,128)S(1)}, s32[1,16]{1,0:T(1,128)}, u32[]{:S(2)}) copy-start(s32[1,16]{1,0:T(1,128)} %param.33) | copy-start | bytes 196
  97.8 6.7 %copy-start.10 = (s32[1,8]{1,0:T(1,128)S(1)}, s32[1,8]{1,0:T(1,128)}, u32[]{:S(2)}) copy-start(s32[1,8]{1,0:T(1,128)} %param.29) | copy-start | bytes 100
  97.8 7.0 %copy-start.5 = (bf16[128,2,512]{2,1,0:T(2,128)(2,1)S(1)}, bf16[128,2,512]{2,1,0:T(2,128)(2,1)}, u32[]{:S(2)}) copy-start(bf16[128,2,512]{2,1,0:T(2,128)(2,1)} %param.35) | copy-start | bytes 786436
  97.8 107.8 %all-to-all-start.1 = ((bf16[16,2,128,512]{3,2,1,0:T(8,128)(2,1)}), bf16[16,2,128,512]{3,2,1,0:T(8,128)(2,1)}, u32[]{:S(2)}, u32[]{:S(2)}) async-start(bf16[16,2,128,512]{3,2,1,0:T(8,128)(2,1)} %broadcast_select_fusion.1), calls=%async_computation.1 | async-start | bytes 8388608 | tf_op jit(solution)/shard_map/all_to_all | solution.py:100
  103.0 2.2 copy-start.11
  103.0 2.2 copy-start.12
  103.0 98.0 %all-reduce.3.cloned.1.call-start = ((), (), s32[]{:S(2)}) async-start(), calls=%async_computation.3 | async-start | bytes 2097152 | tf_op jit(solution)/shard_map/psum | solution.py:175
  104.4 185.8 %all-gather.4.cloned.1.call-start = ((), (), s32[]{:S(2)}) async-start(), calls=%async_computation.4 | async-start | bytes 5242880 | tf_op jit(solution)/shard_map/all_gather | solution.py:22
  210.6 2.9 copy-start.3
  241.2 103.0 %all-gather.6.cloned.1.call-start = ((), (), s32[]{:S(2)}) async-start(), calls=%async_computation.5 | async-start | bytes 5242880 | tf_op jit(solution)/shard_map/all_gather | solution.py:22
  250.7 44.4 %copy-start.4 = (bf16[16,8,4096]{2,1,0:T(8,128)(2,1)S(1)}, bf16[16,8,4096]{2,1,0:T(8,128)(2,1)}, u32[]{:S(2)}) copy-start(bf16[16,8,4096]{2,1,0:T(8,128)(2,1)} %param.23) | copy-start | bytes 3145732
  295.0 168.9 %all-reduce.5.cloned.1.call-start = ((), (), s32[]{:S(2)}) async-start(), calls=%async_computation.6 | async-start | bytes 2097152 | tf_op jit(solution)/shard_map/psum | solution.py:205
  356.2 109.3 %copy-start.7 = (f32[4096]{0:T(1024)S(1)}, f32[4096]{0:T(1024)}, u32[]{:S(2)}) copy-start(f32[4096]{0:T(1024)} %param.21) | copy-start | bytes 49156
  463.9 5.1 %copy-start.2 = (bf16[128,4096]{1,0:T(8,128)(2,1)S(1)}, bf16[128,4096]{1,0:T(8,128)(2,1)}, u32[]{:S(2)}) copy-start(bf16[128,4096]{1,0:T(8,128)(2,1)} %all-reduce.5.cloned.1.call-done) | copy-start | bytes 3145732
  476.3 23.0 %all-to-all-start.2 = ((bf16[32,4,4096]{2,1,0:T(4,128)(2,1)}), bf16[32,4,4096]{2,1,0:T(4,128)(2,1)S(1)}, u32[]{:S(2)}, u32[]{:S(2)}) async-start(bf16[32,4,4096]{2,1,0:T(4,128)(2,1)} %reshape.671), calls=%async_computation.2 | async-start | bytes 2097152 | tf_op jit(solution)/shard_map/all_to_all | solution.py:36
  482.3 18.9 %copy-start.1 = (bf16[256,2048]{1,0:T(8,128)(2,1)S(1)}, bf16[256,2048]{1,0:T(8,128)(2,1)}, u32[]{:S(2)}) copy-start(bf16[256,2048]{1,0:T(8,128)(2,1)} %param.22) | copy-start | bytes 3145732
Sparse Core Ops, SparseCore 0:
  107.0 93.8 all-reduce.2
  241.4 48.7 all-gather.3
  295.1 49.0 all-gather.5
  358.4 105.4 all-reduce.4
where the time goes:
time: 509 us; the launch traced here: 508 us
  waiting for transfers between devices  292 us (57%)
  blocking collectives  73.6 us (14%)
  local copies, waits for them, and re-layouts  47 us (9%)
  other arithmetic  34.5 us (7%)
  matrix products  26.8 us (5%)
  starting transfers between devices  19 us (4%)
  between operations  14.2 us (3%)
    psum x1, waiting for transfers between devices, per_device(): lax.psum(laid.reshape(slots, ranks * width_here).astype(jnp.bfloat16), KV...  106 us
    psum x1, waiting for transfers between devices, per_device(): partial_query, squares = lax.psum((partial_query, squares), KV)  61.1 us
    all_to_all x1, waiting for transfers between devices, move_pages(): lax.all_to_all(outgoing, KV, split_axis=0, concat_axis=0, tiled=True)  59.5 us
    all_gather x2, waiting for transfers between devices, combined_by_axis(): pieces = jax.tree.map(lambda part: lax.all_gather(part, axis), shard)  55.5 us
    all_gather x4, blocking collectives, combined_by_axis(): pieces = jax.tree.map(lambda part: lax.all_gather(part, axis), shard)  39.7 us
    psum x1, blocking collectives, per_device(): partial_query, squares = lax.psum((partial_query, squares), KV)  33.9 us
    all_to_all x1, waiting for transfers between devices, summed_on_arrival(): lax.all_to_all(tiles, axis, split_axis=0, concat_axis=0, tiled=True)  10.6 us
  transfers between devices with their start and end apart: 7, of which 6 were waited for; matrix products, arithmetic and copies ran while one was open for 3% of the time, Pallas kernels for 0%

commit v1 on v0

--- a/solution.py
+++ b/solution.py
@@ -202,7 +202,10 @@
     laid = branch.reshape(slots, ranks, width_here)
     spot = (jnp.arange(ranks, dtype=jnp.int32) == kv_rank) & (tp_rank == 0)
     laid = laid + jnp.where(spot[None, :, None], features[:, None, :], 0.0)
-    resid = lax.psum(laid.reshape(slots, ranks * width_here).astype(jnp.bfloat16), KV_TP)
+    resid = lax.psum(
+        lax.psum(laid.reshape(slots, ranks * width_here).astype(jnp.bfloat16), ("kv_1", "tp")),
+        "kv_0",
+    )
     resid_f = resid.astype(jnp.float32)
     mlp_scale = lax.rsqrt(jnp.sum(resid_f * resid_f, axis=1) / D + norm_eps)
     normed_mlp = (resid_f * mlp_gain).astype(jnp.bfloat16)

time: 509 us -> 515 us (1.012)
    psum x1 -> x2, waiting for transfers between devices: 106 us -> 109 us  [the longest x1 61.2 us: per_device(): lax.psum(laid.reshape(slots, ranks * width_here).astype(jnp.bfloat16), ('...]
  transfers between devices with their start and end apart: 7 -> 8, of which waited for: 6 -> 7; matrix products, arithmetic and copies ran while one was open for 3% -> 3% of each run, Pallas kernels for 0% -> 0%
where the time goes in v1:
time: 515 us; the launch traced here: 514 us
  waiting for transfers between devices  296 us (57%)
  blocking collectives  73.6 us (14%)
  local copies, waits for them, and re-layouts  47 us (9%)
  other arithmetic  34.5 us (7%)
  matrix products  26.8 us (5%)
  starting transfers between devices  22 us (4%)
  between operations  14.2 us (3%)
    psum x1, waiting for transfers between devices, per_device(): lax.psum(laid.reshape(slots, ranks * width_here).astype(jnp.bfloat16), ('...  61.2 us
    psum x1, waiting for transfers between devices, per_device(): partial_query, squares = lax.psum((partial_query, squares), KV)  61.1 us
    all_to_all x1, waiting for transfers between devices, move_pages(): lax.all_to_all(outgoing, KV, split_axis=0, concat_axis=0, tiled=True)  59.5 us
    all_gather x2, waiting for transfers between devices, combined_by_axis(): pieces = jax.tree.map(lambda part: lax.all_gather(part, axis), shard)  55.5 us
    psum x1, waiting for transfers between devices, per_device(): lax.psum(lax.psum(laid.reshape(slots, ranks * width_here).astype(jnp.bflo...  47.8 us
    all_gather x4, blocking collectives, combined_by_axis(): pieces = jax.tree.map(lambda part: lax.all_gather(part, axis), shard)  39.7 us
    psum x1, blocking collectives, per_device(): partial_query, squares = lax.psum((partial_query, squares), KV)  33.9 us
    all_to_all x1, waiting for transfers between devices, summed_on_arrival(): lax.all_to_all(tiles, axis, split_axis=0, concat_axis=0, tiled=True)  10.6 us
  transfers between devices with their start and end apart: 8, of which 7 were waited for; matrix products, arithmetic and copies ran while one was open for 3% of the time, Pallas kernels for 0%

profile of v1, /device:TPU:1, one launch (start us, length us, event | category | flops | bytes accessed | tf_op | source)
XLA Modules:
  0.0 514.1 jit_solution(12943408778276043741)
XLA Ops:
  10.4 5.0 gather_fusion.2
  15.5 4.7 broadcast_select_fusion.2
  20.1 7.6 %all-to-all-start = ((bf16[16,2,128,512]{3,2,1,0:T(8,128)(2,1)}), bf16[16,2,128,512]{3,2,1,0:T(8,128)(2,1)}, u32[]{:S(2)}, u32[]{:S(2)}) async-start(bf16[16,2,128,512]{3,2,1,0:T(8,128)(2,1)} %broadcast_select_fusion.2), calls=%async_computation | async-start | bytes 8388608 | tf_op jit(solution)/shard_map/all_to_all | solution.py:84
  28.5 59.5 %all-to-all-done = bf16[16,2,128,512]{3,2,1,0:T(8,128)(2,1)} async-done(((bf16[16,2,128,512]{3,2,1,0:T(8,128)(2,1)}), bf16[16,2,128,512]{3,2,1,0:T(8,128)(2,1)}, u32[]{:S(2)}, u32[]{:S(2)}) %all-to-all-start) | async-done | bytes 4194336 | tf_op jit(solution)/shard_map/all_to_all | solution.py:84
  88.1 5.0 gather_fusion.3
  93.1 4.7 broadcast_select_fusion.1
  97.8 5.2 %all-to-all-start.1 = ((bf16[16,2,128,512]{3,2,1,0:T(8,128)(2,1)}), bf16[16,2,128,512]{3,2,1,0:T(8,128)(2,1)}, u32[]{:S(2)}, u32[]{:S(2)}) async-start(bf16[16,2,128,512]{3,2,1,0:T(8,128)(2,1)} %broadcast_select_fusion.1), calls=%async_computation.1 | async-start | bytes 8388608 | tf_op jit(solution)/shard_map/all_to_all | solution.py:100
  105.6 33.9 %psum.29 = f32[128]{0:T(128)S(1)} all-reduce(f32[128]{0:T(128)S(1)} %multiply_reduce_fusion.1), channel_id=1, replica_groups=mesh['grp'=4,'kv_0'=4,'kv_1'=4,'tp'=2] {'kv_0','kv_1'}, use_global_device_ids=true, to_apply=%region_2.0 | all-reduce | flops 128 | bytes 1024 | tf_op jit(solution)/shard_map/psum | solution.py:175
  139.8 61.1 %all-reduce.4.cloned.1.call-done = f32[128,2048]{1,0:T(8,128)} async-done(((f32[128,2048]{1,0:T(8,128)}), f32[128,2048]{1,0:T(8,128)}) %all-reduce.4.cloned.1.call-update) | async-done | bytes 1048592 | tf_op jit(solution)/shard_map/psum | solution.py:175
  205.5 5.0 gather_fusion.4
  210.6 2.8 broadcast_select_fusion
  213.4 2.9 pad_maximum_fusion
  216.3 4.7 copy.150
  221.0 4.6 fusion.80
  227.0 4.7 copy.155
  231.7 6.9 %fusion.17 = f32[24,4,4,128]{3,2,1,0:T(4,128)S(1)} fusion(bf16[24,128,4,128]{1,3,2,0:T(8,128)(2,1)} %bitcast.217, f32[24,4,4,128]{3,2,1,0:T(4,128)S(1)} %get-tuple-element.40, f32[24,4,4]{2,1,0:T(4,128)S(1)} %broadcast_select_fusion.3, pred[24,128]{1,0:T(8,128)(4,1)S(1)} %iota_compare_fusion), kind=kOutput, calls=%fused_computation.52 | convolution fusion | flops 75595776 | bytes 3543552 | tf_op jit(solution)/shard_map/ikgt,itkd->ikgd/dot_general | solution.py:134
  241.4 9.3 %all_gather.25 = f32[4,128,16]{1,2,0:T(8,128)S(1)} all-gather(f32[1,128,16]{1,2,0:T(8,128)S(1)} %bitcast.229), channel_id=1, replica_groups=mesh['grp'=4,'kv_0'=4,'kv_1'=4,'tp'=2] {'kv_0'}, dimensions={0}, use_global_device_ids=true | all-gather | bytes 40960 | tf_op jit(solution)/shard_map/all_gather | solution.py:22
  251.3 38.9 %all-gather.4.cloned.1.call-done = f32[4,128,16,128]{3,2,1,0:T(8,128)} async-done(((f32[1,128,16,128]{3,2,1,0:T(8,128)}), f32[4,128,16,128]{3,2,1,0:T(8,128)}) %all-gather.4.cloned.1.call-update) | async-done | bytes 4194320 | tf_op jit(solution)/shard_map/all_gather | solution.py:22
  290.2 4.8 fusion.3
  297.1 9.0 %all-gather = f32[512,16]{0,1:T(8,128)S(1)} all-gather(f32[128,16]{0,1:T(8,128)S(1)} %convolution_add_fusion.1), channel_id=2, replica_groups=mesh['grp'=4,'kv_0'=4,'kv_1'=4,'tp'=2] {'kv_0'}, dimensions={0}, use_global_device_ids=true | all-gather | bytes 40960 | tf_op jit(solution)/shard_map/all_gather | solution.py:22
  306.2 10.8 %all_gather.27 = f32[4,128,16]{1,2,0:T(8,128)S(1)} all-gather(f32[1,128,16]{1,2,0:T(8,128)S(1)} %get-tuple-element.15), channel_id=1, replica_groups=mesh['grp'=4,'kv_0'=4,'kv_1'=4,'tp'=2] {'kv_1'}, dimensions={0}, use_global_device_ids=true | all-gather | bytes 40960 | tf_op jit(solution)/shard_map/all_gather | solution.py:22
  317.0 10.6 %all_gather.30 = f32[4,128,16]{1,2,0:T(8,128)S(1)} all-gather(f32[1,128,16]{1,2,0:T(8,128)S(1)} %get-tuple-element.14), channel_id=1, replica_groups=mesh['grp'=4,'kv_0'=4,'kv_1'=4,'tp'=2] {'kv_1'}, dimensions={0}, use_global_device_ids=true | all-gather | bytes 40960 | tf_op jit(solution)/shard_map/all_gather | solution.py:22
  327.6 16.7 %all-gather.6.cloned.1.call-done = f32[4,128,16,128]{3,2,1,0:T(8,128)} async-done(((f32[1,128,16,128]{3,2,1,0:T(8,128)}), f32[4,128,16,128]{3,2,1,0:T(8,128)}) %all-gather.6.cloned.1.call-update) | async-done | bytes 4194320 | tf_op jit(solution)/shard_map/all_gather | solution.py:22
  344.3 3.9 fusion.78
  350.2 2.6 copy.188
  358.3 61.2 %all-reduce.6.cloned.1.call-done = bf16[128,4096]{1,0:T(8,128)(2,1)} async-done(((bf16[128,4096]{1,0:T(8,128)(2,1)}), bf16[128,4096]{1,0:T(8,128)(2,1)}) %all-reduce.6.cloned.1.call-update) | async-done | bytes 1048592 | tf_op jit(solution)/shard_map/psum | solution.py:206
  419.5 47.8 %all-reduce.8.cloned.1.call-done = bf16[128,4096]{1,0:T(8,128)(2,1)} async-done(((bf16[128,4096]{1,0:T(8,128)(2,1)}), bf16[128,4096]{1,0:T(8,128)(2,1)}) %all-reduce.8.cloned.1.call-update) | async-done | bytes 1048592 | tf_op jit(solution)/shard_map/psum | solution.py:205
  468.9 3.5 convolution_multiply_fusion.1
  472.4 6.0 %convolution_convert_fusion = bf16[128,4096]{1,0:T(8,128)(2,1)S(1)} fusion(bf16[448,4096]{1,0:T(8,128)(2,1)} %param.26, bf16[4096,448]{0,1:T(8,128)(2,1)} %param.25, f32[4096]{0:T(1024)S(1)} %copy-done.7, bf16[128,4096]{1,0:T(8,128)(2,1)S(1)} %copy-done.2, f32[128,448]{0,1:T(8,128)S(1)} %convolution_multiply_fusion.1, f32[128]{0:T(128)S(1)} %add_rsqrt_fusion), kind=kOutput, calls=%fused_computation.7 | convolution fusion | flops 942022656 | bytes 9683456 | tf_op jit(solution)/shard_map/dot_general | solution.py:217
  479.6 9.0 %all-to-all-start.2 = ((bf16[32,4,4096]{2,1,0:T(4,128)(2,1)}), bf16[32,4,4096]{2,1,0:T(4,128)(2,1)S(1)}, u32[]{:S(2)}, u32[]{:S(2)}) async-start(bf16[32,4,4096]{2,1,0:T(4,128)(2,1)} %reshape.671), calls=%async_computation.2 | async-start | bytes 2097152 | tf_op jit(solution)/shard_map/all_to_all | solution.py:36
  488.7 4.8 fusion.92
  495.0 10.6 %all-to-all-done.2 = bf16[32,4,4096]{2,1,0:T(4,128)(2,1)S(1)} async-done(((bf16[32,4,4096]{2,1,0:T(4,128)(2,1)}), bf16[32,4,4096]{2,1,0:T(4,128)(2,1)S(1)}, u32[]{:S(2)}, u32[]{:S(2)}) %all-to-all-start.2) | async-done | bytes 1048608 | tf_op jit(solution)/shard_map/all_to_all | solution.py:36
  (124 shorter events, 32.1 us)
Async XLA Ops:
  7.2 95.8 %copy-start = (bf16[256,2048]{1,0:T(8,128)(2,1)S(1)}, bf16[256,2048]{1,0:T(8,128)(2,1)}, u32[]{:S(2)}) copy-start(bf16[256,2048]{1,0:T(8,128)(2,1)} %param.22) | copy-start | bytes 3145732
  20.1 68.0 %all-to-all-start = ((bf16[16,2,128,512]{3,2,1,0:T(8,128)(2,1)}), bf16[16,2,128,512]{3,2,1,0:T(8,128)(2,1)}, u32[]{:S(2)}, u32[]{:S(2)}) async-start(bf16[16,2,128,512]{3,2,1,0:T(8,128)(2,1)} %broadcast_select_fusion.2), calls=%async_computation | async-start | bytes 8388608 | tf_op jit(solution)/shard_map/all_to_all | solution.py:84
  97.8 5.3 %copy-start.6 = (bf16[128,256]{1,0:T(8,128)(2,1)S(1)}, bf16[128,256]{1,0:T(8,128)(2,1)}, u32[]{:S(2)}) copy-start(bf16[128,256]{1,0:T(8,128)(2,1)} %param.19) | copy-start | bytes 196612
  97.8 5.3 %copy-start.8 = (f32[256]{0:T(256)S(1)}, f32[256]{0:T(256)}, u32[]{:S(2)}) copy-start(f32[256]{0:T(256)} %param.20) | copy-start | bytes 3076
  97.8 6.7 %copy-start.9 = (s32[1,16]{1,0:T(1,128)S(1)}, s32[1,16]{1,0:T(1,128)}, u32[]{:S(2)}) copy-start(s32[1,16]{1,0:T(1,128)} %param.33) | copy-start | bytes 196
  97.8 6.7 %copy-start.10 = (s32[1,8]{1,0:T(1,128)S(1)}, s32[1,8]{1,0:T(1,128)}, u32[]{:S(2)}) copy-start(s32[1,8]{1,0:T(1,128)} %param.29) | copy-start | bytes 100
  97.8 7.0 %copy-start.5 = (bf16[128,2,512]{2,1,0:T(2,128)(2,1)S(1)}, bf16[128,2,512]{2,1,0:T(2,128)(2,1)}, u32[]{:S(2)}) copy-start(bf16[128,2,512]{2,1,0:T(2,128)(2,1)} %param.35) | copy-start | bytes 786436
  97.8 107.8 %all-to-all-start.1 = ((bf16[16,2,128,512]{3,2,1,0:T(8,128)(2,1)}), bf16[16,2,128,512]{3,2,1,0:T(8,128)(2,1)}, u32[]{:S(2)}, u32[]{:S(2)}) async-start(bf16[16,2,128,512]{3,2,1,0:T(8,128)(2,1)} %broadcast_select_fusion.1), calls=%async_computation.1 | async-start | bytes 8388608 | tf_op jit(solution)/shard_map/all_to_all | solution.py:100
  103.0 2.2 copy-start.11
  103.0 2.2 copy-start.12
  103.0 98.0 %all-reduce.4.cloned.1.call-start = ((), (), s32[]{:S(2)}) async-start(), calls=%async_computation.3 | async-start | bytes 2097152 | tf_op jit(solution)/shard_map/psum | solution.py:175
  104.4 185.8 %all-gather.4.cloned.1.call-start = ((), (), s32[]{:S(2)}) async-start(), calls=%async_computation.4 | async-start | bytes 5242880 | tf_op jit(solution)/shard_map/all_gather | solution.py:22
  210.6 2.9 copy-start.3
  241.2 103.0 %all-gather.6.cloned.1.call-start = ((), (), s32[]{:S(2)}) async-start(), calls=%async_computation.5 | async-start | bytes 5242880 | tf_op jit(solution)/shard_map/all_gather | solution.py:22
  250.7 44.4 %copy-start.4 = (bf16[16,8,4096]{2,1,0:T(8,128)(2,1)S(1)}, bf16[16,8,4096]{2,1,0:T(8,128)(2,1)}, u32[]{:S(2)}) copy-start(bf16[16,8,4096]{2,1,0:T(8,128)(2,1)} %param.23) | copy-start | bytes 3145732
  295.0 124.5 %all-reduce.6.cloned.1.call-start = ((), (), s32[]{:S(2)}) async-start(), calls=%async_computation.6 | async-start | bytes 2097152 | tf_op jit(solution)/shard_map/psum | solution.py:206
  356.2 112.7 %copy-start.7 = (f32[4096]{0:T(1024)S(1)}, f32[4096]{0:T(1024)}, u32[]{:S(2)}) copy-start(f32[4096]{0:T(1024)} %param.21) | copy-start | bytes 49156
  358.2 109.0 %all-reduce.8.cloned.1.call-start = ((), (), s32[]{:S(2)}) async-start(), calls=%async_computation.7 | async-start | bytes 2097152 | tf_op jit(solution)/shard_map/psum | solution.py:205
  467.3 5.1 copy-start.2
  479.6 25.9 %all-to-all-start.2 = ((bf16[32,4,4096]{2,1,0:T(4,128)(2,1)}), bf16[32,4,4096]{2,1,0:T(4,128)(2,1)S(1)}, u32[]{:S(2)}, u32[]{:S(2)}) async-start(bf16[32,4,4096]{2,1,0:T(4,128)(2,1)} %reshape.671), calls=%async_computation.2 | async-start | bytes 2097152 | tf_op jit(solution)/shard_map/all_to_all | solution.py:36
  488.6 18.9 %copy-start.1 = (bf16[256,2048]{1,0:T(8,128)(2,1)S(1)}, bf16[256,2048]{1,0:T(8,128)(2,1)}, u32[]{:S(2)}) copy-start(bf16[256,2048]{1,0:T(8,128)(2,1)} %param.22) | copy-start | bytes 3145732
Sparse Core Ops, SparseCore 0:
  107.0 93.8 all-reduce.3
  241.4 48.7 all-gather.3
  295.1 49.0 all-gather.5
  358.4 61.0 all-reduce.5
  421.7 45.5 all-reduce.7
